TPU v7x, 32 devices: a whole 2x2x4 slice. The times are simulated.
32 devices in a mesh: expert: 4 (over x, core), shard: 8 (over z, y).
Axes of the slice: x: 2, y: 2, z: 4, core: 2. Of those that a mesh axis runs over, the one named last changes fastest.
Arguments:
- master_gate: float32 [64, 2048, 1024], P('expert', 'shard'), may hold values from -0.1875 to 0.1875
- master_up: float32 [64, 2048, 1024], P('expert', 'shard'), may hold values from -0.1875 to 0.1875
- master_down: float32 [64, 1024, 2048], P('expert', None, 'shard'), may hold values from -0.25 to 0.25
- router_weight: float32 [2048, 64], P('shard', 'expert'), may hold values from -0.125 to 0.125
- router_gain: float32 [2048], P('shard'), may hold values from 0.25 to 1.75
Outputs:
- final_gate: bfloat16 [64, 2048, 1024], P('expert', None, 'shard')
- final_up: bfloat16 [64, 2048, 1024], P('expert', None, 'shard')
- final_down: bfloat16 [64, 1024, 2048], P('expert', 'shard')
- scale_gate: float32 [64, 1024], P('expert', 'shard')
- scale_up: float32 [64, 1024], P('expert', 'shard')
- scale_down: float32 [64, 1024], P('expert', 'shard')
- serve_router: bfloat16 [2048, 64], replicated
All inputs are finite; a program needn't handle non-finite values.
Results may differ from a plain program's by a relative error of at most 0.001.
Values may be sent and summed in bfloat16 or wider, within the bound.
A program may use at most 192 MiB of HBM per device.

v0:
```python
import jax
import jax.numpy as jnp
from jax import lax
from jax.sharding import PartitionSpec as P


def on_device(master_gate, master_up, master_down, router_weight, router_gain):
    total_gate, total_up, total_down = lax.psum(
        (
            jnp.sum(master_gate * master_gate, axis=1),
            jnp.sum(master_up * master_up, axis=1),
            jnp.sum(master_down * master_down, axis=2),
        ),
        "shard",
    )
    scale_gate = jnp.sqrt(total_gate)
    scale_up = jnp.sqrt(total_up)
    scale_down = jnp.sqrt(total_down)
    narrow_gate, narrow_up, narrow_down = (
        (master_gate / jnp.expand_dims(scale_gate, 1)).astype(jnp.bfloat16),
        (master_up / jnp.expand_dims(scale_up, 1)).astype(jnp.bfloat16),
        (master_down / jnp.expand_dims(scale_down, 2)).astype(jnp.bfloat16),
    )
    final_gate, final_up = (
        lax.all_to_all(narrow_gate, "shard", split_axis=2, concat_axis=1, tiled=True),
        lax.all_to_all(narrow_up, "shard", split_axis=2, concat_axis=1, tiled=True),
    )
    final_down = lax.all_to_all(narrow_down, "shard", split_axis=1, concat_axis=2, tiled=True)
    scale_gate = lax.dynamic_slice_in_dim(
        scale_gate, lax.axis_index("shard") * final_gate.shape[2], final_gate.shape[2], axis=1
    )
    scale_up = lax.dynamic_slice_in_dim(
        scale_up, lax.axis_index("shard") * final_up.shape[2], final_up.shape[2], axis=1
    )
    scale_down = lax.dynamic_slice_in_dim(
        scale_down, lax.axis_index("shard") * final_down.shape[1], final_down.shape[1], axis=1
    )
    part_router = (router_weight * router_gain[:, None]).astype(jnp.bfloat16)
    row_router = lax.all_gather(part_router, "shard", axis=0, tiled=True)
    serve_router = lax.all_gather(row_router, "expert", axis=1, tiled=True)
    return (final_gate, final_up, final_down, scale_gate, scale_up, scale_down, serve_router)


def solution(mesh):
    placed = (
        P("expert", "shard", None),
        P("expert", "shard", None),
        P("expert", None, "shard"),
        P("shard", "expert"),
        P("shard"),
    )
    return jax.shard_map(
        on_device,
        mesh=mesh,
        in_specs=placed,
        out_specs=(
            P("expert", None, "shard"),
            P("expert", None, "shard"),
            P("expert", "shard", None),
            P("expert", "shard"),
            P("expert", "shard"),
            P("expert", "shard"),
            P(),
        ),
        check_vma=False,
    )
```

profile of v0, /device:TPU:0, one launch (start us, length us, event | category | flops | bytes accessed | tf_op | source)
XLA Modules:
  0.0 758.6 jit_solution(1279384502401970627)
XLA Ops:
  7.2 0.0 all-reduce.3.cloned.1.call-start
  7.2 8.6 %multiply_reduce_fusion = f32[16,1024]{1,0:T(8,128)} fusion(f32[16,1024,256]{2,1,0:T(8,128)} %param.7), kind=kLoop, calls=%fused_computation.2 | loop fusion | flops 8372224 | bytes 16842752 | tf_op jit(solution)/shard_map/reduce_sum | solution.py:12
  15.8 12.6 %multiply_reduce_fusion.1 = (f32[16,1024]{1,0:T(8,128)}, f32[16,1024]{1,0:T(8,128)}) fusion(f32[16,256,1024]{2,1,0:T(8,128)} %param.6, f32[16,256,1024]{2,1,0:T(8,128)} %param.5), kind=kLoop, calls=%fused_computation.4 | loop fusion | flops 16744448 | bytes 33685504 | tf_op jit(solution)/shard_map/reduce_sum | solution.py:11
  28.4 0.0 all-reduce.3.cloned.1.call-update
  28.4 17.6 %copy.19 = f32[16,256,1024]{1,0,2:T(8,128)} copy(f32[16,256,1024]{2,1,0:T(8,128)} %param.6) | data formatting | bytes 33554432 | tf_op args[1]
  46.0 56.7 %all-reduce.3.cloned.1.call-done = (f32[16,1024]{1,0:T(8,128)}, f32[16,1024]{1,0:T(8,128)}, f32[16,1024]{1,0:T(8,128)}) async-done(((f32[16,1024]{1,0:T(8,128)}, f32[16,1024]{1,0:T(8,128)}, f32[16,1024]{1,0:T(8,128)}), (f32[16,1024]{1,0:T(8,128)}, f32[16,1024]{1,0:T(8,128)}, f32[16,1024]{1,0:T(8,128)})) %all-reduce.3.cloned.1.call-update) | async-done | bytes 196624 | tf_op jit(solution)/shard_map/psum | solution.py:8
  102.7 0.9 sqrt.10
  103.6 0.2 copy.18
  103.8 9.6 %divide_convert_fusion = bf16[16,256,1024]{1,0,2:T(8,128)(2,1)} fusion(f32[16,256,1024]{1,0,2:T(8,128)} %copy.19, f32[16,1024]{0,1:T(8,128)S(1)} %copy.18), kind=kLoop, calls=%fused_computation.3 | loop fusion | flops 8388608 | bytes 25231360 | tf_op jit(solution)/shard_map/convert_element_type | solution.py:21
  113.4 4.9 all-to-all-start.1
  118.4 0.0 copy-start.1
  118.4 17.6 %copy.16 = f32[16,256,1024]{1,0,2:T(8,128)} copy(f32[16,256,1024]{2,1,0:T(8,128)} %param.5) | data formatting | bytes 33554432 | tf_op args[0]
  136.0 0.0 copy-done.1
  136.0 0.2 copy.15
  136.2 0.0 copy-start
  136.2 9.7 %divide_convert_fusion.1 = bf16[16,256,1024]{1,0,2:T(8,128)(2,1)} fusion(f32[16,256,1024]{1,0,2:T(8,128)} %copy.16, f32[16,1024]{0,1:T(8,128)S(1)} %copy.15), kind=kLoop, calls=%fused_computation.5 | loop fusion | flops 8388608 | bytes 25231360 | tf_op jit(solution)/shard_map/convert_element_type | solution.py:20
  145.9 153.8 %all-to-all-done.1 = bf16[16,256,1024]{1,0,2:T(8,128)(2,1)} async-done(((bf16[16,256,1024]{1,0,2:T(8,128)(2,1)}), bf16[16,256,1024]{1,0,2:T(8,128)(2,1)}, u32[]{:S(2)}, u32[]{:S(2)}) %all-to-all-start.1) | async-done | bytes 8388640 | tf_op jit(solution)/shard_map/all_to_all | solution.py:26
  299.7 4.9 all-to-all-start
  304.7 0.0 copy-done
  304.7 0.2 copy.21
  304.9 0.0 copy-start.2
  304.9 0.0 copy-start.3
  305.0 16.6 %fusion = bf16[16,1024,256]{2,0,1:T(8,128)(2,1)} fusion(f32[16,1024,256]{2,1,0:T(8,128)} %param.7, f32[16,1024]{0,1:T(8,128)S(1)} %copy.21), kind=kLoop, calls=%fused_computation.1 | loop fusion | flops 8388608 | bytes 25231360 | tf_op jit(solution)/shard_map/convert_element_type | solution.py:22
  321.6 165.1 %all-to-all-done = bf16[16,256,1024]{1,0,2:T(8,128)(2,1)} async-done(((bf16[16,256,1024]{1,0,2:T(8,128)(2,1)}), bf16[16,256,1024]{1,0,2:T(8,128)(2,1)}, u32[]{:S(2)}, u32[]{:S(2)}) %all-to-all-start) | async-done | bytes 8388640 | tf_op jit(solution)/shard_map/all_to_all | solution.py:25
  486.7 5.0 all-to-all-start.2
  491.7 0.0 copy-done.2
  491.8 0.0 copy-done.3
  491.8 202.1 %all_gather.6 = bf16[2048,16]{0,1:T(8,128)(2,1)S(1)} all-gather(bf16[256,16]{0,1:T(8,128)(2,1)S(1)} %multiply_convert_fusion), channel_id=1, replica_groups=mesh['expert'=4,'shard'=8] {'shard'}, dimensions={0}, use_global_device_ids=true | all-gather | bytes 73728 | tf_op jit(solution)/shard_map/all_gather | solution.py:39
  693.9 5.9 all_gather.7
  699.9 0.6 constant_dynamic-slice_fusion
  700.5 0.6 constant_dynamic-slice_fusion.1
  701.1 0.6 constant_dynamic-slice_fusion.2
  701.7 12.3 %copy.20 = bf16[16,8,256,128]{3,2,1,0:T(8,128)(2,1)} copy(bf16[16,8,256,128]{2,0,3,1:T(8,128)(2,1)} %bitcast.4) | data formatting | bytes 16777216 | tf_op jit(solution)/shard_map/all_to_all | solution.py:26
  713.9 12.3 %copy.17 = bf16[16,8,256,128]{3,2,1,0:T(8,128)(2,1)} copy(bf16[16,8,256,128]{2,0,3,1:T(8,128)(2,1)} %bitcast.1) | data formatting | bytes 16777216 | tf_op jit(solution)/shard_map/all_to_all | solution.py:25
  726.2 0.0 all-to-all-done.2
  726.2 11.4 %copy.23 = bf16[16,128,8,256]{3,2,1,0:T(8,128)(2,1)} copy(bf16[16,128,8,256]{3,0,1,2:T(8,128)(2,1)} %bitcast.7) | data formatting | bytes 16777216 | tf_op jit(solution)/shard_map/all_to_all | solution.py:28
  737.6 13.4 %all_to_all.50 = bf16[16,128,2048]{2,1,0:T(8,128)(2,1)} reshape(bf16[16,128,8,256]{3,2,1,0:T(8,128)(2,1)} %copy.23) | data formatting | bytes 16777216 | tf_op jit(solution)/shard_map/all_to_all | solution.py:28
  751.0 0.7 copy.31
  (3 shorter events, 0.0 us)
Async XLA Ops:
  7.2 95.5 %all-reduce.3.cloned.1.call-start = ((), (), s32[]{:S(2)}) async-start(), calls=%async_computation.3 | async-start | bytes 393216 | tf_op jit(solution)/shard_map/psum | solution.py:8
  113.4 186.3 %all-to-all-start.1 = ((bf16[16,256,1024]{1,0,2:T(8,128)(2,1)}), bf16[16,256,1024]{1,0,2:T(8,128)(2,1)}, u32[]{:S(2)}, u32[]{:S(2)}) async-start(bf16[16,256,1024]{1,0,2:T(8,128)(2,1)} %divide_convert_fusion), calls=%async_computation.1 | async-start | bytes 16777216 | tf_op jit(solution)/shard_map/all_to_all | solution.py:26
  118.4 17.6 %copy-start.1 = (f32[16,1024]{1,0:T(8,128)S(1)}, f32[16,1024]{1,0:T(8,128)}, u32[]{:S(2)}) copy-start(f32[16,1024]{1,0:T(8,128)} %get-tuple-element.7) | copy-start | bytes 196612
  136.2 168.5 %copy-start = (f32[16,1024]{1,0:T(8,128)S(1)}, f32[16,1024]{1,0:T(8,128)}, u32[]{:S(2)}) copy-start(f32[16,1024]{1,0:T(8,128)} %get-tuple-element.9) | copy-start | bytes 196612
  299.7 187.0 %all-to-all-start = ((bf16[16,256,1024]{1,0,2:T(8,128)(2,1)}), bf16[16,256,1024]{1,0,2:T(8,128)(2,1)}, u32[]{:S(2)}, u32[]{:S(2)}) async-start(bf16[16,256,1024]{1,0,2:T(8,128)(2,1)} %divide_convert_fusion.1), calls=%async_computation | async-start | bytes 16777216 | tf_op jit(solution)/shard_map/all_to_all | solution.py:25
  304.9 186.8 %copy-start.2 = (f32[256,16]{0,1:T(8,128)S(1)}, f32[256,16]{0,1:T(8,128)}, u32[]{:S(2)}) copy-start(f32[256,16]{0,1:T(8,128)} %param.8) | copy-start | bytes 49156
  304.9 186.8 %copy-start.3 = (f32[256]{0:T(256)S(1)}, f32[256]{0:T(256)}, u32[]{:S(2)}) copy-start(f32[256]{0:T(256)} %param.9) | copy-start | bytes 3076
  486.7 239.5 %all-to-all-start.2 = ((bf16[16,1024,256]{2,0,1:T(8,128)(2,1)}), bf16[16,1024,256]{2,0,1:T(8,128)(2,1)}, u32[]{:S(2)}, u32[]{:S(2)}) async-start(bf16[16,1024,256]{2,0,1:T(8,128)(2,1)} %fusion), calls=%async_computation.2 | async-start | bytes 16777216 | tf_op jit(solution)/shard_map/all_to_all | solution.py:28
Sparse Core Ops, SparseCore 0:
  28.6 74.0 all-reduce.2
where the time goes:
time: 760 us; the launch traced here: 759 us
  waiting for transfers between devices  376 us (49%)
  blocking collectives  208 us (27%)
  local copies, waits for them, and re-layouts  88.6 us (12%)
  other arithmetic  57.2 us (8%)
  starting transfers between devices  14.9 us (2%)
  between operations  14.2 us (2%)
    all_gather x1, blocking collectives, on_device(): row_router = lax.all_gather(part_router, 'shard', axis=0, tiled=True)  202 us
    all_to_all x1, waiting for transfers between devices, on_device(): lax.all_to_all(narrow_gate, 'shard', split_axis=2, concat_axis=1, tiled=T...  165 us
    all_to_all x1, waiting for transfers between devices, on_device(): lax.all_to_all(narrow_up, 'shard', split_axis=2, concat_axis=1, tiled=True)  154 us
    psum x1, waiting for transfers between devices, on_device(): lax.psum((jnp.sum(master_gate * master_gate, axis=1), jnp.sum(master_up *...  56.7 us
    unnamed x11, local copies, waits for them, and re-layouts  35.9 us
    all_to_all x2, local copies, waits for them, and re-layouts, on_device(): lax.all_to_all(narrow_down, 'shard', split_axis=1, concat_axis=2, tiled=T...  24.8 us
    convert_element_type x1, other arithmetic, on_device(): (master_down / jnp.expand_dims(scale_down, 2)).astype(jnp.bfloat16)  16.6 us
  transfers between devices with their start and end apart: 4, of which 3 were waited for; matrix products, arithmetic and copies ran while one was open for 12% of the time, Pallas kernels for 0%

commit v1 on v0

--- a/solution.py
+++ b/solution.py
@@ -1,10 +1,215 @@
+import functools
+
 import jax
 import jax.numpy as jnp
 from jax import lax
+from jax.experimental import pallas as pl
+from jax.experimental.pallas import tpu as pltpu
 from jax.sharding import PartitionSpec as P
 
-
-def on_device(master_gate, master_up, master_down, router_weight, router_gain):
+MESH = pl.DeviceIdType.MESH
+SLOTS = 4
+
+
+def exchange(
+    n, groups, gate, up, down, weight, gain,
+    out_gate, out_up, out_down, scale_gate, scale_up, scale_down, out_router,
+    in_gate, in_up, in_down, send_gate, send_up, send_down,
+    part, arrived, owned, inverse, narrow_router,
+    load_sem, part_send, part_recv, inv_send, inv_recv,
+    big_send, big_recv, own_sem, router_sem,
+):
+    experts, rows, width = gate.shape
+    cols = width // n
+    me = lax.axis_index("shard")
+    grp = lax.axis_index("expert")
+    order = sorted(range(1, n), key=lambda k: (abs(2 * k - n), k))
+    lanes = min(128, down.shape[2])
+
+    def peer(k):
+        return lax.rem(me + k, n)
+
+    def load(t):
+        slot = lax.rem(t, SLOTS)
+        return [
+            pltpu.make_async_copy(src.at[t], dst.at[slot], load_sem.at[slot, i])
+            for i, (src, dst) in enumerate(((gate, in_gate), (up, in_up), (down, in_down)))
+        ]
+
+    for copy in load(0):
+        copy.start()
+
+    barrier = pltpu.get_barrier_semaphore()
+    for k in range(1, n):
+        pl.semaphore_signal(barrier, inc=1, device_id={"shard": peer(k)}, device_id_type=MESH)
+    for k in range(1, groups):
+        pl.semaphore_signal(
+            barrier, inc=1, device_id={"expert": lax.rem(grp + k, groups)}, device_id_type=MESH
+        )
+
+    w = weight[...]
+    experts_here, depth = w.shape
+    narrow_router[...] = (w * gain[...]).astype(jnp.bfloat16)
+    router_rows = pl.ds(pl.multiple_of(grp * experts_here, experts_here), experts_here)
+    router_cols = pl.ds(pl.multiple_of(me * depth, depth), depth)
+
+    pl.semaphore_wait(barrier, n - 1 + groups - 1)
+
+    def router_first(k):
+        return pltpu.make_async_remote_copy(
+            src_ref=narrow_router,
+            dst_ref=out_router.at[router_rows, router_cols],
+            send_sem=router_sem.at[0],
+            recv_sem=router_sem.at[1],
+            device_id={"shard": peer(k)},
+            device_id_type=MESH,
+        )
+
+    router_own = pltpu.make_async_copy(
+        narrow_router, out_router.at[router_rows, router_cols], router_sem.at[2]
+    )
+
+    def router_second(k):
+        return pltpu.make_async_remote_copy(
+            src_ref=out_router.at[router_rows, :],
+            dst_ref=out_router.at[router_rows, :],
+            send_sem=router_sem.at[3],
+            recv_sem=router_sem.at[4],
+            device_id={"expert": lax.rem(grp + k, groups)},
+            device_id_type=MESH,
+        )
+
+    def sums(t):
+        @pl.when(t + 1 < experts)
+        def _():
+            for copy in load(t + 1):
+                copy.start()
+
+        for copy in load(t):
+            copy.wait()
+        slot = lax.rem(t, SLOTS)
+        for i, ref in enumerate((in_gate, in_up)):
+            for d in range(n):
+                x = ref[slot, :, d * cols:(d + 1) * cols]
+                part[t, d, i] = jnp.sum(x * x, axis=0, keepdims=True)
+        for d in range(n):
+            x = in_down[slot, d * cols:(d + 1) * cols, :]
+            x = x * x
+            folded = x[:, :lanes]
+            for c in range(lanes, x.shape[1], lanes):
+                folded = folded + x[:, c:c + lanes]
+            part[t, d, 2] = jnp.sum(folded.T, axis=0, keepdims=True)
+        for k in order:
+            pltpu.make_async_remote_copy(
+                src_ref=part.at[t, peer(k)],
+                dst_ref=arrived.at[t, k - 1],
+                send_sem=part_send,
+                recv_sem=part_recv.at[t],
+                device_id={"shard": peer(k)},
+                device_id_type=MESH,
+            ).start()
+
+    def reduce(t):
+        pltpu.make_async_copy(arrived.at[t], arrived.at[t], part_recv.at[t]).wait()
+        for i, out in enumerate((scale_gate, scale_up, scale_down)):
+            total = part[t, me, i]
+            for k in range(n - 1):
+                total = total + arrived[t, k, i]
+            scale = jnp.sqrt(total)
+            out[pl.ds(t, 1), :] = scale
+            owned[t, i] = 1.0 / scale
+            inverse[t, me, i] = 1.0 / scale
+        for k in order:
+            pltpu.make_async_remote_copy(
+                src_ref=owned.at[t],
+                dst_ref=inverse.at[t, me],
+                send_sem=inv_send,
+                recv_sem=inv_recv.at[t],
+                device_id={"shard": peer(k)},
+                device_id_type=MESH,
+            ).start()
+
+    row_at = pl.ds(pl.multiple_of(me * rows, rows), rows)
+    col_at = pl.ds(pl.multiple_of(me * down.shape[2], down.shape[2]), down.shape[2])
+
+    def places(t):
+        return (
+            (send_gate, out_gate.at[t, row_at, :]),
+            (send_up, out_up.at[t, row_at, :]),
+            (send_down, out_down.at[t, :, col_at]),
+        )
+
+    def finish(t):
+        pltpu.make_async_copy(
+            inverse.at[t, pl.ds(0, n - 1)], inverse.at[t, pl.ds(0, n - 1)], inv_recv.at[t]
+        ).wait()
+        slot = lax.rem(t, SLOTS)
+        for i, (ref, send) in enumerate(((in_gate, send_gate), (in_up, send_up))):
+            for d in range(n):
+                x = ref[slot, :, d * cols:(d + 1) * cols]
+                send[t, d] = (x * inverse[t, d, i]).astype(jnp.bfloat16)
+        for d in range(n):
+            across = jnp.broadcast_to(inverse[t, d, 2], (lanes, cols)).T
+            for c in range(0, down.shape[2], lanes):
+                x = in_down[slot, d * cols:(d + 1) * cols, c:c + lanes]
+                send_down[t, d, :, c:c + lanes] = (x * across).astype(jnp.bfloat16)
+        for i, (send, place) in enumerate(places(t)):
+            for k in order:
+                pltpu.make_async_remote_copy(
+                    src_ref=send.at[t, peer(k)],
+                    dst_ref=place,
+                    send_sem=big_send.at[i],
+                    recv_sem=big_recv.at[i],
+                    device_id={"shard": peer(k)},
+                    device_id_type=MESH,
+                ).start()
+            pltpu.make_async_copy(send.at[t, me], place, own_sem.at[i]).start()
+
+    def step(t, carry):
+        @pl.when(t < experts)
+        def _():
+            sums(t)
+
+        @pl.when(t == 0)
+        def _():
+            router_own.start()
+            for k in order:
+                router_first(k).start()
+
+        @pl.when((t >= 1) & (t <= experts))
+        def _():
+            reduce(t - 1)
+
+        @pl.when(t >= 2)
+        def _():
+            finish(t - 2)
+
+        return carry
+
+    lax.fori_loop(0, experts + 2, step, 0)
+
+    router_own.wait()
+    gathered = out_router.at[router_rows, pl.ds(0, (n - 1) * depth)]
+    pltpu.make_async_copy(gathered, gathered, router_sem.at[1]).wait()
+    for k in range(1, groups):
+        router_second(k).start()
+
+    others = pl.ds(0, n - 1)
+    for i, send in enumerate((send_gate, send_up, send_down)):
+        blocks = send.at[:, others]
+        pltpu.make_async_copy(blocks, blocks, big_recv.at[i]).wait()
+        pltpu.make_async_copy(blocks, blocks, big_send.at[i]).wait()
+        mine = send.at[:, 0]
+        pltpu.make_async_copy(mine, mine, own_sem.at[i]).wait()
+    pltpu.make_async_copy(arrived, arrived, part_send).wait()
+    pltpu.make_async_copy(inverse.at[:, others], inverse.at[:, others], inv_send).wait()
+    pltpu.make_async_copy(gathered, gathered, router_sem.at[0]).wait()
+    handed = out_router.at[pl.ds(0, (groups - 1) * experts_here), :]
+    pltpu.make_async_copy(handed, handed, router_sem.at[3]).wait()
+    pltpu.make_async_copy(handed, handed, router_sem.at[4]).wait()
+
+
+def by_collectives(master_gate, master_up, master_down, router_weight, router_gain):
     total_gate, total_up, total_down = lax.psum(
         (
             jnp.sum(master_gate * master_gate, axis=1),
@@ -41,6 +246,59 @@
     return (final_gate, final_up, final_down, scale_gate, scale_up, scale_down, serve_router)
 
 
+def on_device(n, groups, gate, up, down, router_weight, router_gain):
+    experts, rows, width = gate.shape
+    cols = width // n
+    inner = down.shape[2]
+    depth, experts_here = router_weight.shape
+    if cols % 128 or inner % 128 or depth % 128:
+        return by_collectives(gate, up, down, router_weight, router_gain)
+    narrow, wide = jnp.bfloat16, jnp.float32
+    dma = pltpu.SemaphoreType.DMA
+    any_space = pl.BlockSpec(memory_space=pl.ANY)
+    vmem = pl.BlockSpec(memory_space=pltpu.VMEM)
+    outs = pl.pallas_call(
+        functools.partial(exchange, n, groups),
+        out_shape=(
+            jax.ShapeDtypeStruct((experts, rows * n, cols), narrow),
+            jax.ShapeDtypeStruct((experts, rows * n, cols), narrow),
+            jax.ShapeDtypeStruct((experts, cols, inner * n), narrow),
+            jax.ShapeDtypeStruct((experts, cols), wide),
+            jax.ShapeDtypeStruct((experts, cols), wide),
+            jax.ShapeDtypeStruct((experts, cols), wide),
+            jax.ShapeDtypeStruct((experts_here * groups, depth * n), narrow),
+        ),
+        in_specs=[any_space] * 3 + [vmem] * 2,
+        out_specs=(any_space,) * 3 + (vmem,) * 3 + (any_space,),
+        scratch_shapes=[
+            pltpu.VMEM((SLOTS, rows, width), wide),
+            pltpu.VMEM((SLOTS, rows, width), wide),
+            pltpu.VMEM((SLOTS, width, inner), wide),
+            pltpu.VMEM((experts, n, rows, cols), narrow),
+            pltpu.VMEM((experts, n, rows, cols), narrow),
+            pltpu.VMEM((experts, n, cols, inner), narrow),
+            pltpu.VMEM((experts, n, 3, 1, cols), wide),
+            pltpu.VMEM((experts, n - 1, 3, 1, cols), wide),
+            pltpu.VMEM((experts, 3, 1, cols), wide),
+            pltpu.VMEM((experts, n, 3, 1, cols), wide),
+            pltpu.VMEM((experts_here, depth), narrow),
+            dma((SLOTS, 3)),
+            dma,
+            dma((experts,)),
+            dma,
+            dma((experts,)),
+            dma((3,)),
+            dma((3,)),
+            dma((3,)),
+            dma((5,)),
+        ],
+        compiler_params=pltpu.CompilerParams(
+            collective_id=0, has_side_effects=True, vmem_limit_bytes=60 * 2**20
+        ),
+    )(gate, up, down, router_weight.T, router_gain[None, :])
+    return outs[:6] + (outs[6].T,)
+
+
 def solution(mesh):
     placed = (
         P("expert", "shard", None),
@@ -50,7 +308,7 @@
         P("shard"),
     )
     return jax.shard_map(
-        on_device,
+        functools.partial(on_device, mesh.shape["shard"], mesh.shape["expert"]),
         mesh=mesh,
         in_specs=placed,
         out_specs=(

time: 760 us -> 589 us (0.78)
  Pallas kernels: 0 us -> 562 us
  waiting for transfers between devices: 376 us -> 0 us
  blocking collectives: 208 us -> 0 us
  local copies, waits for them, and re-layouts: 88.6 us -> 26.2 us
  other arithmetic: 57.2 us -> 0 us
  starting transfers between devices: 14.9 us -> 0 us
  between operations: 14.2 us -> 0.65 us
    pallas_call x0 -> x1, Pallas kernels: none -> 562 us  [on_device(): pl.pallas_call(functools.partial(exchange, n, groups), out_shape=(jax.Sha...]
    all_to_all x3 -> x0, waiting for transfers between devices: 319 us -> none  [the longest x1 165 us: on_device(): lax.all_to_all(narrow_gate, 'shard', split_axis=2, concat_axis=1, tiled=T...]
    all_gather x2 -> x0, blocking collectives: 208 us -> none  [the longest x1 202 us: on_device(): row_router = lax.all_gather(part_router, 'shard', axis=0, tiled=True)]
    psum x1 -> x0, waiting for transfers between devices: 56.7 us -> none  [on_device(): lax.psum((jnp.sum(master_gate * master_gate, axis=1), jnp.sum(master_up *...]
    all_to_all x4 -> x0, local copies, waits for them, and re-layouts: 49.4 us -> none  [the longest x2 24.8 us: on_device(): lax.all_to_all(narrow_down, 'shard', split_axis=1, concat_axis=2, tiled=T...]
    convert_element_type x4 -> x0, other arithmetic: 36 us -> none  [the longest x1 16.6 us: on_device(): (master_down / jnp.expand_dims(scale_down, 2)).astype(jnp.bfloat16)]
    reduce_sum x2 -> x0, other arithmetic: 21.2 us -> none  [the longest x1 12.6 us: on_device(): jnp.sum(master_up * master_up, axis=1)]
    all_to_all x3 -> x0, starting transfers between devices: 14.9 us -> none  [the longest x1 5.01 us: on_device(): lax.all_to_all(narrow_down, 'shard', split_axis=1, concat_axis=2, tiled=T...]
  transfers between devices with their start and end apart: 4 -> 0, of which waited for: 3 -> 0; matrix products, arithmetic and copies ran while one was open for 12% -> 0% of each run, Pallas kernels for 0% -> 0%
where the time goes in v1:
time: 589 us
  Pallas kernels  562 us (95%)
  local copies, waits for them, and re-layouts  26.2 us (4%)
    pallas_call x1, Pallas kernels, on_device(): pl.pallas_call(functools.partial(exchange, n, groups), out_shape=(jax.Sha...  562 us
    unnamed x15, local copies, waits for them, and re-layouts  26.2 us

profile of v1, /device:TPU:0, one launch (start us, length us, event | category | flops | bytes accessed | tf_op | source)
XLA Modules:
  0.0 588.6 jit_solution(16323457185139764811)
XLA Ops:
  0.6 561.8 %shard_map.108 = (bf16[16,2048,128]{2,1,0:T(8,128)(2,1)}, bf16[16,2048,128]{2,1,0:T(8,128)(2,1)}, bf16[16,128,2048]{2,1,0:T(8,128)(2,1)}, f32[16,128]{1,0:T(8,12...) custom-call(f32[16,256,1024]{2,1,0:T(8,128)} %gate.1, f32[16,256,1024]{2,1,0:T(8,128)} %up.1, ...), custom_call_target="tpu_custom_call" | custom-call | tf_op jit(solution)/shard_map/pallas_call | solution.py:260
  562.4 7.6 %copy.19 = bf16[16,2048,128]{2,1,0:T(8,128)(2,1)} copy(bf16[16,2048,128]{2,1,0:T(8,128)(2,1)} %get-tuple-element.28) | data formatting | bytes 16777216
  570.0 7.6 %copy.20 = bf16[16,2048,128]{2,1,0:T(8,128)(2,1)} copy(bf16[16,2048,128]{2,1,0:T(8,128)(2,1)} %get-tuple-element.29) | data formatting | bytes 16777216
  577.6 0.0 copy-start.3
  577.6 0.0 copy-start.2
  577.6 0.0 copy-start.1
  577.6 0.0 copy-start
  577.6 8.5 %copy.21 = bf16[16,128,2048]{2,1,0:T(8,128)(2,1)} copy(bf16[16,128,2048]{2,1,0:T(8,128)(2,1)} %get-tuple-element.30) | data formatting | bytes 16777216
  586.1 0.0 copy-done.3
  586.1 0.6 copy.22
  586.7 0.0 copy-done.2
  586.7 0.6 copy.23
  587.3 0.0 copy-done.1
  587.3 0.6 copy.24
  587.9 0.0 copy-done
  587.9 0.7 copy.25
Async XLA Ops:
  577.6 8.5 %copy-start.3 = (f32[16,128]{1,0:T(8,128)S(1)}, f32[16,128]{1,0:T(8,128)}, u32[]{:S(2)}) copy-start(f32[16,128]{1,0:T(8,128)} %get-tuple-element.31) | copy-start | bytes 24580
  577.6 9.1 %copy-start.2 = (f32[16,128]{1,0:T(8,128)S(1)}, f32[16,128]{1,0:T(8,128)}, u32[]{:S(2)}) copy-start(f32[16,128]{1,0:T(8,128)} %get-tuple-element.32) | copy-start | bytes 24580
  577.6 9.7 %copy-start.1 = (f32[16,128]{1,0:T(8,128)S(1)}, f32[16,128]{1,0:T(8,128)}, u32[]{:S(2)}) copy-start(f32[16,128]{1,0:T(8,128)} %get-tuple-element.33) | copy-start | bytes 24580
  577.6 10.3 %copy-start = (bf16[64,2048]{1,0:T(8,128)(2,1)S(1)}, bf16[64,2048]{1,0:T(8,128)(2,1)}, u32[]{:S(2)}) copy-start(bf16[64,2048]{1,0:T(8,128)(2,1)} %get-tuple-element.20) | copy-start | bytes 786436

commit v2 on v1

--- a/solution.py
+++ b/solution.py
@@ -13,13 +13,14 @@
 
 def exchange(
     n, groups, gate, up, down, weight, gain,
-    out_gate, out_up, out_down, scale_gate, scale_up, scale_down, out_router,
+    out_gate, out_up, out_down, scale_gate, scale_up, scale_down, out_router, later,
     in_gate, in_up, in_down, send_gate, send_up, send_down,
     part, arrived, owned, inverse, narrow_router,
     load_sem, part_send, part_recv, inv_send, inv_recv,
     big_send, big_recv, own_sem, router_sem,
 ):
     experts, rows, width = gate.shape
+    early = out_down.shape[0]
     cols = width // n
     me = lax.axis_index("shard")
     grp = lax.axis_index("expert")
@@ -132,38 +133,43 @@
     row_at = pl.ds(pl.multiple_of(me * rows, rows), rows)
     col_at = pl.ds(pl.multiple_of(me * down.shape[2], down.shape[2]), down.shape[2])
 
-    def places(t):
-        return (
-            (send_gate, out_gate.at[t, row_at, :]),
-            (send_up, out_up.at[t, row_at, :]),
-            (send_down, out_down.at[t, :, col_at]),
-        )
+    def spread(t, i, send, place):
+        for k in order:
+            pltpu.make_async_remote_copy(
+                src_ref=send.at[t, peer(k)],
+                dst_ref=place,
+                send_sem=big_send.at[i],
+                recv_sem=big_recv.at[i],
+                device_id={"shard": peer(k)},
+                device_id_type=MESH,
+            ).start()
+        pltpu.make_async_copy(send.at[t, me], place, own_sem.at[i]).start()
 
     def finish(t):
         pltpu.make_async_copy(
             inverse.at[t, pl.ds(0, n - 1)], inverse.at[t, pl.ds(0, n - 1)], inv_recv.at[t]
         ).wait()
         slot = lax.rem(t, SLOTS)
-        for i, (ref, send) in enumerate(((in_gate, send_gate), (in_up, send_up))):
+        for i, (ref, send, out) in enumerate(
+            ((in_gate, send_gate, out_gate), (in_up, send_up, out_up))
+        ):
             for d in range(n):
                 x = ref[slot, :, d * cols:(d + 1) * cols]
                 send[t, d] = (x * inverse[t, d, i]).astype(jnp.bfloat16)
+            spread(t, i, send, out.at[t, row_at, :])
         for d in range(n):
             across = jnp.broadcast_to(inverse[t, d, 2], (lanes, cols)).T
             for c in range(0, down.shape[2], lanes):
                 x = in_down[slot, d * cols:(d + 1) * cols, c:c + lanes]
                 send_down[t, d, :, c:c + lanes] = (x * across).astype(jnp.bfloat16)
-        for i, (send, place) in enumerate(places(t)):
-            for k in order:
-                pltpu.make_async_remote_copy(
-                    src_ref=send.at[t, peer(k)],
-                    dst_ref=place,
-                    send_sem=big_send.at[i],
-                    recv_sem=big_recv.at[i],
-                    device_id={"shard": peer(k)},
-                    device_id_type=MESH,
-                ).start()
-            pltpu.make_async_copy(send.at[t, me], place, own_sem.at[i]).start()
+
+        @pl.when(t < early)
+        def _():
+            spread(t, 2, send_down, out_down.at[t, :, col_at])
+
+        @pl.when(t >= early)
+        def _():
+            pltpu.make_async_copy(send_down.at[t], later.at[:, t - early], own_sem.at[3]).start()
 
     def step(t, carry):
         @pl.when(t < experts)
@@ -195,11 +201,14 @@
         router_second(k).start()
 
     others = pl.ds(0, n - 1)
-    for i, send in enumerate((send_gate, send_up, send_down)):
-        blocks = send.at[:, others]
+    pltpu.make_async_copy(later, later, own_sem.at[3]).wait()
+    for i, (send, sent) in enumerate(
+        ((send_gate, experts), (send_up, experts), (send_down, early))
+    ):
+        blocks = send.at[pl.ds(0, sent), others]
         pltpu.make_async_copy(blocks, blocks, big_recv.at[i]).wait()
         pltpu.make_async_copy(blocks, blocks, big_send.at[i]).wait()
-        mine = send.at[:, 0]
+        mine = send.at[pl.ds(0, sent), 0]
         pltpu.make_async_copy(mine, mine, own_sem.at[i]).wait()
     pltpu.make_async_copy(arrived, arrived, part_send).wait()
     pltpu.make_async_copy(inverse.at[:, others], inverse.at[:, others], inv_send).wait()
@@ -254,6 +263,7 @@
     if cols % 128 or inner % 128 or depth % 128:
         return by_collectives(gate, up, down, router_weight, router_gain)
     narrow, wide = jnp.bfloat16, jnp.float32
+    early = experts - max(1, experts // 8)
     dma = pltpu.SemaphoreType.DMA
     any_space = pl.BlockSpec(memory_space=pl.ANY)
     vmem = pl.BlockSpec(memory_space=pltpu.VMEM)
@@ -262,14 +272,15 @@
         out_shape=(
             jax.ShapeDtypeStruct((experts, rows * n, cols), narrow),
             jax.ShapeDtypeStruct((experts, rows * n, cols), narrow),
-            jax.ShapeDtypeStruct((experts, cols, inner * n), narrow),
+            jax.ShapeDtypeStruct((early, cols, inner * n), narrow),
             jax.ShapeDtypeStruct((experts, cols), wide),
             jax.ShapeDtypeStruct((experts, cols), wide),
             jax.ShapeDtypeStruct((experts, cols), wide),
             jax.ShapeDtypeStruct((experts_here * groups, depth * n), narrow),
+            jax.ShapeDtypeStruct((n, experts - early, cols, inner), narrow),
         ),
         in_specs=[any_space] * 3 + [vmem] * 2,
-        out_specs=(any_space,) * 3 + (vmem,) * 3 + (any_space,),
+        out_specs=(any_space,) * 3 + (vmem,) * 3 + (any_space,) * 2,
         scratch_shapes=[
             pltpu.VMEM((SLOTS, rows, width), wide),
             pltpu.VMEM((SLOTS, rows, width), wide),
@@ -289,14 +300,70 @@
             dma((experts,)),
             dma((3,)),
             dma((3,)),
-            dma((3,)),
+            dma((4,)),
             dma((5,)),
         ],
         compiler_params=pltpu.CompilerParams(
             collective_id=0, has_side_effects=True, vmem_limit_bytes=60 * 2**20
         ),
     )(gate, up, down, router_weight.T, router_gain[None, :])
-    return outs[:6] + (outs[6].T,)
+    late = lax.all_to_all(outs[7], "shard", split_axis=0, concat_axis=0, tiled=True)
+
+    def one(shape, cap):
+        block = (1,) + shape[1:]
+        return pl.BlockSpec(block, lambda t: (jnp.minimum(t, cap - 1), 0, 0))
+
+    specs = [
+        one(outs[0].shape, experts),
+        one(outs[1].shape, experts),
+        one(outs[2].shape, early),
+    ] + [pl.BlockSpec(x.shape, lambda t: (0, 0)) for x in outs[3:7]]
+    full = jax.ShapeDtypeStruct((experts, cols, inner * n), narrow)
+    moved = sum(x.size * x.dtype.itemsize for x in outs[:7])
+    placed = pl.pallas_call(
+        place,
+        grid=(experts,),
+        in_specs=specs,
+        out_specs=specs,
+        out_shape=tuple(
+            full if i == 2 else jax.ShapeDtypeStruct(x.shape, x.dtype)
+            for i, x in enumerate(outs[:7])
+        ),
+        compiler_params=pltpu.CompilerParams(dimension_semantics=("arbitrary",)),
+        cost_estimate=pl.CostEstimate(flops=0, bytes_accessed=2 * moved, transcendentals=0),
+    )(*outs[:7])
+    final_down = pl.pallas_call(
+        functools.partial(place_late, n, early),
+        in_specs=[any_space] * 2,
+        out_specs=any_space,
+        out_shape=full,
+        input_output_aliases={0: 0},
+        scratch_shapes=[dma((n,))],
+        compiler_params=pltpu.CompilerParams(vmem_limit_bytes=2**20),
+    )(placed[2], late)
+    return placed[:2] + (final_down,) + placed[3:6] + (placed[6].T,)
+
+
+def place(*refs):
+    half = len(refs) // 2
+    for src, dst in zip(refs[:half], refs[half:]):
+        dst[...] = src[...]
+
+
+def place_late(n, early, _, late, out, sem):
+    inner = late.shape[3]
+    copies = [
+        pltpu.make_async_copy(
+            late.at[d],
+            out.at[pl.ds(early, late.shape[1]), :, pl.ds(d * inner, inner)],
+            sem.at[d],
+        )
+        for d in range(n)
+    ]
+    for copy in copies:
+        copy.start()
+    for copy in copies:
+        copy.wait()
 
 
 def solution(mesh):

time: 589 us -> 571 us (0.969)
  local copies, waits for them, and re-layouts: 26.2 us -> 0 us
    unnamed x15 -> x0, local copies, waits for them, and re-layouts: 26.2 us -> none
    pallas_call x1, Pallas kernels: 562 us -> 539 us  [on_device(): pl.pallas_call(functools.partial(exchange, n, groups), out_shape=(jax.Sha...]
    pallas_call x0 -> x2, Pallas kernels: none -> 22.7 us  [the longest x1 21.7 us: on_device(): pl.pallas_call(place, grid=(experts,), in_specs=specs, out_specs=specs, o...]
  transfers between devices with their start and end apart: 0 -> 1, of which waited for: 0 -> 1; matrix products, arithmetic and copies ran while one was open for 0% -> 0% of each run, Pallas kernels for 0% -> 4%
where the time goes in v2:
time: 571 us; the launch traced here: 570 us
  Pallas kernels  562 us (98%)
    pallas_call x1, Pallas kernels, on_device(): pl.pallas_call(functools.partial(exchange, n, groups), out_shape=(jax.Sha...  539 us
    pallas_call x1, Pallas kernels, on_device(): pl.pallas_call(place, grid=(experts,), in_specs=specs, out_specs=specs, o...  21.7 us
  transfers between devices with their start and end apart: 1, of which 1 were waited for; matrix products, arithmetic and copies ran while one was open for 0% of the time, Pallas kernels for 4%

profile of v2, /device:TPU:0, one launch (start us, length us, event | category | flops | bytes accessed | tf_op | source)
XLA Modules:
  0.0 570.0 jit_solution(12858681172371220265)
XLA Ops:
  0.6 539.1 %shard_map.108 = (bf16[16,2048,128]{2,1,0:T(8,128)(2,1)}, bf16[16,2048,128]{2,1,0:T(8,128)(2,1)}, bf16[14,128,2048]{2,1,0:T(8,128)(2,1)}, f32[16,128]{1,0:T(8,12...) custom-call(f32[16,256,1024]{2,1,0:T(8,128)} %gate.1, ...), custom_call_target="tpu_custom_call" | custom-call | tf_op jit(solution)/shard_map/pallas_call | solution.py:270
  539.7 4.5 all-to-all-start
  544.2 21.7 %shard_map.109 = (bf16[16,2048,128]{2,1,0:T(8,128)(2,1)}, bf16[16,2048,128]{2,1,0:T(8,128)(2,1)}, bf16[16,128,2048]{2,1,0:T(8,128)(2,1)}, f32[16,128]{1,0:T(8,12...) custom-call(bf16[16,2048,128]{2,1,0:T(8,128)(2,1)} %get-tuple-element.22.refs_0_, ...), custom_call_target="tpu_custom_call" | custom-call | bytes 48807936 | tf_op jit(solution)/shard_map/pallas_call | solution.py:323
  565.9 3.1 all-to-all-done.late
  569.0 1.0 shard_map.110
Async XLA Ops:
  539.7 29.2 %all-to-all-start = ((bf16[8,2,128,256]{3,2,1,0:T(8,128)(2,1)}), bf16[8,2,128,256]{3,2,1,0:T(8,128)(2,1)S(1)}, u32[]{:S(2)}, u32[]{:S(2)}) async-start(bf16[8,2,128,256]{3,2,1,0:T(8,128)(2,1)} %get-tuple-element.32), calls=%async_computation | async-start | bytes 2097152 | tf_op jit(solution)/shard_map/all_to_all | solution.py:310
